TPU v7x, 8 devices: a whole 2x2x1 slice. The times are simulated.
8 devices in a mesh: dp: 1 (over z), tp: 8 (over y, x, core).
Axes of the slice: x: 2, y: 2, z: 1, core: 2. Of those that a mesh axis runs over, the one named last changes fastest.
Arguments:
- x_in: bfloat16 [32, 512, 3072], P('dp')
- adapter_ids: int32 [32], P('dp')
- gain_attn: float32 [3072], replicated
- gain_mlp: float32 [3072], replicated
- w_q: bfloat16 [3072, 24, 128], P(None, 'tp')
- w_k: bfloat16 [3072, 8, 128], P(None, 'tp')
- w_v: bfloat16 [3072, 8, 128], P(None, 'tp')
- w_o: bfloat16 [24, 128, 3072], P('tp')
- w_gate: bfloat16 [3072, 8192], P(None, 'tp')
- w_up: bfloat16 [3072, 8192], P(None, 'tp')
- w_down: bfloat16 [8192, 3072], P('tp')
- a_q: bfloat16 [16, 3072, 8], P(None, None, 'tp')
- b_q: bfloat16 [16, 8, 24, 128], P(None, None, 'tp')
- a_k: bfloat16 [16, 3072, 8], P(None, None, 'tp')
- b_k: bfloat16 [16, 8, 8, 128], P(None, None, 'tp')
- a_v: bfloat16 [16, 3072, 8], P(None, None, 'tp')
- b_v: bfloat16 [16, 8, 8, 128], P(None, None, 'tp')
- a_o: bfloat16 [16, 24, 128, 8], P(None, 'tp')
- b_o: bfloat16 [16, 8, 3072], P(None, None, 'tp')
- a_gate: bfloat16 [16, 3072, 8], P(None, None, 'tp')
- b_gate: bfloat16 [16, 8, 8192], P(None, None, 'tp')
- a_up: bfloat16 [16, 3072, 8], P(None, None, 'tp')
- b_up: bfloat16 [16, 8, 8192], P(None, None, 'tp')
- a_down: bfloat16 [16, 8192, 8], P(None, 'tp')
- b_down: bfloat16 [16, 8, 3072], P(None, None, 'tp')
Outputs:
- output: bfloat16 [32, 512, 3072], P('dp')
All inputs are finite; a program needn't handle non-finite values.
Results may differ from a plain program's by a relative error of at most 0.02.
Values are sent between devices in bfloat16 or wider.
A program may use at most 1 GiB of HBM per device.

v0:
```python
import jax
import jax.numpy as jnp
from jax import lax
from jax.sharding import PartitionSpec as P

value_a10 = 16
RMS_EPS = 1e-5


def rms_scale(x_in, gain_vec):
    x_f32 = x_in.astype(jnp.float32)
    inv_rms = lax.rsqrt(jnp.mean(x_f32 * x_f32, axis=-1, keepdims=True) + RMS_EPS)
    return (x_f32 * inv_rms * gain_vec).astype(jnp.bfloat16)


def causal_attention(q_flat, k_flat, v_flat, kv_heads, head_dim):
    num_seqs, seq_len = q_flat.shape[0], q_flat.shape[1]
    q_group = q_flat.reshape(num_seqs, seq_len, kv_heads, -1, head_dim)
    k_group = k_flat.reshape(num_seqs, seq_len, kv_heads, head_dim)
    v_group = v_flat.reshape(num_seqs, seq_len, kv_heads, head_dim)
    scores = jnp.einsum('bqngd,bknd->bngqk', q_group, k_group, preferred_element_type=jnp.float32) * head_dim ** -0.5
    causal = jnp.arange(seq_len)[:, None] >= jnp.arange(seq_len)[None, :]
    prob_bf = jax.nn.softmax(jnp.where(causal, scores, -jnp.inf), axis=-1).astype(jnp.bfloat16)
    att_out = jnp.einsum('bngqk,bknd->bqngd', prob_bf, v_group, preferred_element_type=jnp.float32)
    return att_out.astype(jnp.bfloat16).reshape(num_seqs, seq_len, -1)


def column_proj(h_in, w_loc, a_sel, b_sel, scale):
    value_a9 = jnp.einsum('bsd,bdr->bsr', h_in, a_sel, preferred_element_type=jnp.float32).astype(jnp.bfloat16)
    value_a8 = lax.all_gather(value_a9, 'tp', axis=2, tiled=True)
    base_out = jnp.einsum('bsd,de->bse', h_in, w_loc, preferred_element_type=jnp.float32)
    array_b8 = jnp.einsum('bsr,bre->bse', value_a8, b_sel, preferred_element_type=jnp.float32)
    return (base_out + scale * array_b8).astype(jnp.bfloat16)


def row_proj(h_in, w_loc, a_sel, b_sel, scale, resid_full):
    base_part = jnp.einsum('bse,ed->bsd', h_in, w_loc, preferred_element_type=jnp.float32).astype(jnp.bfloat16)
    value_a9 = jnp.einsum('bse,ber->bsr', h_in, a_sel, preferred_element_type=jnp.float32).astype(jnp.bfloat16)
    base_sum = lax.psum_scatter(base_part, 'tp', scatter_dimension=2, tiled=True)
    value_a8 = lax.psum(value_a9, 'tp')
    width = base_sum.shape[2]
    resid_loc = lax.dynamic_slice_in_dim(resid_full, lax.axis_index('tp') * width, width, axis=2)
    array_b8 = jnp.einsum('bsr,brd->bsd', value_a8, b_sel, preferred_element_type=jnp.float32)
    out_loc = resid_loc.astype(jnp.float32) + base_sum.astype(jnp.float32) + scale * array_b8
    return lax.all_gather(out_loc.astype(jnp.bfloat16), 'tp', axis=2, tiled=True)


def solution(mesh):
    act_spec = P('dp', None, None)
    w_head_spec = P(None, 'tp', None)
    w_out_spec = P('tp', None, None)
    w_col_spec = P(None, 'tp')
    w_row_spec = P('tp', None)
    a_rank_spec = P(None, None, 'tp')
    b_head_spec = P(None, None, 'tp', None)
    b_col_spec = P(None, None, 'tp')
    a_head_spec = P(None, 'tp', None, None)
    a_row_spec = P(None, 'tp', None)
    in_specs = (act_spec, P('dp'), P(None), P(None), w_head_spec, w_head_spec, w_head_spec, w_out_spec,
                w_col_spec, w_col_spec, w_row_spec, a_rank_spec, b_head_spec, a_rank_spec, b_head_spec,
                a_rank_spec, b_head_spec, a_head_spec, b_col_spec, a_rank_spec, b_col_spec,
                a_rank_spec, b_col_spec, a_row_spec, b_col_spec)

    def local_layer(x_in, adapter_ids, gain_attn, gain_mlp, w_q, w_k, w_v, w_o, w_gate, w_up, w_down,
                    a_q, b_q, a_k, b_k, a_v, b_v, a_o, b_o, a_gate, b_gate, a_up, b_up, a_down, b_down):
        num_seqs, model_dim = x_in.shape[0], x_in.shape[2]
        rank = b_q.shape[1]
        scale = value_a10 / rank

        def per_sequence(stack):
            return jnp.take(stack, adapter_ids, axis=0)

        def column(h_in, w_loc, a_stack, b_stack):
            return column_proj(h_in, w_loc.reshape(model_dim, -1), per_sequence(a_stack),
                               per_sequence(b_stack).reshape(num_seqs, rank, -1), scale)

        h_norm = rms_scale(x_in, gain_attn)
        q_loc = column(h_norm, w_q, a_q, b_q)
        k_loc = column(h_norm, w_k, a_k, b_k)
        v_loc = column(h_norm, w_v, a_v, b_v)
        att_loc = causal_attention(q_loc, k_loc, v_loc, w_k.shape[1], w_k.shape[2])
        x_one = row_proj(att_loc, w_o.reshape(-1, model_dim), per_sequence(a_o).reshape(num_seqs, -1, rank),
                         per_sequence(b_o), scale, x_in)
        h_two = rms_scale(x_one, gain_mlp)
        gate_loc = column(h_two, w_gate, a_gate, b_gate)
        up_loc = column(h_two, w_up, a_up, b_up)
        mlp_mid = (jax.nn.silu(gate_loc.astype(jnp.float32)) * up_loc.astype(jnp.float32)).astype(jnp.bfloat16)
        return row_proj(mlp_mid, w_down, per_sequence(a_down), per_sequence(b_down), scale, x_one)

    return jax.shard_map(local_layer, mesh=mesh, in_specs=in_specs, out_specs=act_spec, check_vma=False)
```

profile of v0, /device:TPU:0, one launch (start us, length us, event | category | flops | bytes accessed | tf_op | source)
XLA Modules:
  0.0 3265.4 jit_solution(6711236062647286390)
XLA Ops:
  8.8 1.8 gather_fusion.3
  10.6 1.8 gather_fusion.5
  12.4 1.8 gather_fusion.7
  14.1 1.8 gather_fusion.9
  15.9 1.8 gather_fusion.11
  17.7 30.8 fusion
  50.1 36.4 %fusion.50 = bf16[32,1,512]{2,1,0:T(2,128)(2,1)S(1)} fusion(bf16[32,3072,1]{1,0,2:T(8,128)(2,1)} %get-tuple-element.10, bf16[32,512,3072]{2,1,0:T(8,128)(2,1)} %param.33, f32[3072]{0:T(1024)} %param.35, f32[32,512]{1,0:T(8,128)} %add_rsqrt_fusion.1), kind=kOutput, calls=%fused_computation.78 | convolution fusion | flops 301989888 | bytes 100970496 | tf_op jit(solution)/shard_map/bsd,bdr->bsr/dot_general | solution.py:29
  86.5 14.4 all_gather.23
  102.2 4.3 copy.57
  106.5 36.4 %fusion.52 = bf16[32,1,512]{2,1,0:T(2,128)(2,1)S(1)} fusion(bf16[32,3072,1]{1,0,2:T(8,128)(2,1)S(1)} %get-tuple-element.8, bf16[32,512,3072]{2,1,0:T(8,128)(2,1)} %param.33, f32[3072]{0:T(1024)S(1)} %copy-done.39, f32[32,512]{1,0:T(8,128)S(1)} %copy-done.34), kind=kOutput, calls=%fused_computation.80 | convolution fusion | flops 301989888 | bytes 100970496 | tf_op jit(solution)/shard_map/bsd,bdr->bsr/dot_general | solution.py:29
  142.9 11.8 all_gather.22
  155.9 40.3 %fusion.34 = f32[32,512,128]{2,1,0:T(8,128)} fusion(bf16[3072,1,128]{2,0,1:T(8,128)(2,1)} %param.38, bf16[32,512,3072]{2,1,0:T(8,128)(2,1)} %param.33, f32[3072]{0:T(1024)S(1)} %copy-done.39, f32[32,512]{1,0:T(8,128)S(1)} %copy-done.34), kind=kOutput, calls=%fused_computation.63 | convolution fusion | flops 13086228480 | bytes 109916160 | tf_op jit(solution)/shard_map/bsd,de->bse/dot_general | solution.py:31
  196.2 36.5 %fusion.54 = bf16[32,1,512]{2,1,0:T(2,128)(2,1)S(1)} fusion(bf16[32,3072,1]{1,0,2:T(8,128)(2,1)S(1)} %copy-done.31, bf16[32,512,3072]{2,1,0:T(8,128)(2,1)} %param.33, f32[3072]{0:T(1024)S(1)} %copy-done.39, f32[32,512]{1,0:T(8,128)S(1)} %copy-done.34), kind=kOutput, calls=%fused_computation.82 | convolution fusion | flops 301989888 | bytes 100970496 | tf_op jit(solution)/shard_map/bsd,bdr->bsr/dot_general | solution.py:29
  232.7 12.0 all_gather.21
  245.9 1.3 gather_fusion.1
  247.2 10.9 fusion.58
  258.1 52.3 %add_convert_fusion.4 = bf16[32,512,384]{1,2,0:T(8,128)(2,1)} fusion(f32[32,512,384]{1,2,0:T(8,128)} %fusion.58, bf16[3072,384,1]{0,1,2:T(8,128)(2,1)} %bitcast.197, bf16[32,512,3072]{2,1,0:T(8,128)(2,1)} %param.33, f32[3072]{0:T(1024)S(1)} %copy-done.40, f32[32,512]{1,0:T(8,128)S(1)} %copy-done.35), kind=kOutput, calls=%fused_computation.45 | convolution fusion | flops 38874906624 | bytes 140849152 | tf_op jit(solution)/shard_map/bsd,de->bse/dot_general | solution.py:31
  310.4 41.7 %fusion.7 = (f32[32,3,512]{2,1,0:T(4,128)S(1)}, f32[32,512,512,3]{2,1,3,0:T(8,128)}) fusion(pred[512,512]{0,1:T(8,128)(4,1)S(1)} %copy-done.6, bf16[32,512,3,128]{1,3,2,0:T(8,128)(2,1)} %bitcast.194, f32[32,512,128]{2,1,0:T(8,128)} %fusion.34, bf16[32,512,8]{1,0,2:T(8,128)(2,1)S(1)} %copy-done.15, bf16[32,8,128]{2,1,0:T(8,128)(2,1)S(1)} %copy-done.29, ...), kind=kOutput, calls=%fused_computation.30 | convolution fusion | flops 6557777920 | bytes 122421280 | tf_op jit(solution)/shard_map/bqngd,bknd->bngqk/dot_general | solution.py:21
  352.1 32.3 fusion.6
  384.4 4.7 fusion.62
  389.1 41.2 %fusion.148 = bf16[32,512,128,1]{2,1,3,0:T(8,128)(2,1)} fusion(f32[32,512,128]{2,1,0:T(8,128)} %fusion.62, bf16[3072,1,128]{2,0,1:T(8,128)(2,1)} %param.39, bf16[32,512,3072]{2,1,0:T(8,128)(2,1)} %param.33, f32[3072]{0:T(1024)S(1)} %copy-done.40, f32[32,512]{1,0:T(8,128)S(1)} %copy-done.35), kind=kOutput, calls=%fused_computation.53.clone.clone.2 | convolution fusion | flops 13092519936 | bytes 114110464 | tf_op jit(solution)/shard_map/bsd,de->bse/dot_general | solution.py:31
  430.3 42.2 %fusion.16 = bf16[32,128,3,512]{3,1,2,0:T(8,128)(2,1)} fusion(f32[32,3,512]{2,1,0:T(4,128)S(1)} %copy-done.28, f32[32,3,512]{2,1,0:T(4,128)S(1)} %get-tuple-element.14, f32[32,512,512,3]{2,1,3,0:T(8,128)} %get-tuple-element.15, pred[512,512]{0,1:T(8,128)(4,1)S(1)} %copy-done.6, bf16[32,512,128,1]{2,1,3,0:T(8,128)(2,1)} %fusion.148), kind=kOutput, calls=%fused_computation.48 | convolution fusion | flops 6574571520 | bytes 118095872 | tf_op jit(solution)/shard_map/bngqk,bknd->bqngd/dot_general | solution.py:24
  472.4 7.1 convolution_convert_fusion.3
  479.6 63.5 %convolution_convert_fusion.1 = bf16[32,512,3072]{1,2,0:T(8,128)(2,1)} fusion(bf16[32,512,384]{1,2,0:T(8,128)(2,1)} %bitcast.196, bf16[384,3072,1]{1,0,2:T(8,128)(2,1)S(1)} %bitcast.188), kind=kOutput, calls=%fused_computation.39 | convolution fusion | flops 38705037312 | bytes 115605504 | tf_op jit(solution)/shard_map/bse,ed->bsd/dot_general | solution.py:37
  544.6 10.7 constant_dynamic-slice_fusion
  555.3 16.7 copy.97
  572.0 501.8 %reduce-scatter.3.cloned.1.call-done = bf16[32,512,384]{1,2,0:T(8,128)(2,1)} async-done(((bf16[32,512,3072]{1,2,0:T(8,128)(2,1)}), bf16[32,512,384]{1,2,0:T(8,128)(2,1)}) %reduce-scatter.3.cloned.1.call-update) | async-done | bytes 12582928 | tf_op jit(solution)/shard_map/reduce_scatter | solution.py:39
  1073.8 16.7 add_convert_fusion.3
  1090.6 1.4 gather_fusion.12
  1092.0 1.4 gather_fusion.10
  1093.4 1.4 gather_fusion.2
  1094.8 436.1 %all-gather.3.cloned.1.call-done = bf16[32,512,3072]{1,2,0:T(8,128)(2,1)} async-done(((bf16[32,512,384]{1,2,0:T(8,128)(2,1)}), bf16[32,512,3072]{1,2,0:T(8,128)(2,1)}) %all-gather.3.cloned.1.call-update) | async-done | bytes 100663312 | tf_op jit(solution)/shard_map/all_gather | solution.py:45
  1530.8 30.8 fusion.3
  1561.6 65.6 %fusion.5 = bf16[32,512,3072]{1,2,0:T(8,128)(2,1)} fusion(bf16[32,512,3072]{1,2,0:T(8,128)(2,1)} %all-gather.3.cloned.1.call-done, f32[3072]{0:T(1024)S(1)} %copy-done.38, f32[32,512]{1,0:T(8,128)S(1)} %add_rsqrt_fusion), kind=kLoop, calls=%fused_computation.23 | loop fusion | flops 201326592 | bytes 201404416 | tf_op jit(solution)/shard_map/convert_element_type | solution.py:13
  1627.2 31.7 fusion.46
  1659.0 11.6 all_gather.26
  1670.6 31.7 fusion.48
  1702.3 11.6 all_gather.25
  1713.9 116.5 %fusion.21 = f32[32,512,1024]{2,1,0:T(8,128)} fusion(bf16[32,512,3072]{1,2,0:T(8,128)(2,1)} %fusion.5, bf16[3072,1024]{1,0:T(8,128)(2,1)} %param.41), kind=kOutput, calls=%fused_computation.51 | convolution fusion | flops 103079215104 | bytes 174063616 | tf_op jit(solution)/shard_map/bsd,de->bse/dot_general | solution.py:31
  1830.5 23.3 fusion.38
  1853.8 23.2 fusion.40
  1876.9 135.3 %fusion.12 = bf16[32,512,1024]{2,1,0:T(8,128)(2,1)} fusion(f32[32,512,1024]{2,1,0:T(8,128)} %fusion.21, f32[32,512,1024]{2,1,0:T(8,128)} %fusion.40, f32[32,512,1024]{2,1,0:T(8,128)} %fusion.38, bf16[32,512,3072]{1,2,0:T(8,128)(2,1)} %fusion.5, bf16[3072,1024]{1,0:T(8,128)(2,1)} %param.42), kind=kOutput, calls=%fused_computation.37 | convolution fusion | flops 103314096128 | bytes 341835776 | tf_op jit(solution)/shard_map/bsd,de->bse/dot_general | solution.py:31
  2012.3 14.8 convolution_convert_fusion.2
  2027.1 114.8 %convolution_convert_fusion = bf16[32,512,3072]{1,2,0:T(8,128)(2,1)} fusion(bf16[32,512,1024]{2,1,0:T(8,128)(2,1)} %fusion.12, bf16[1024,3072]{1,0:T(8,128)(2,1)} %param.43), kind=kOutput, calls=%fused_computation.38 | convolution fusion | flops 103129546752 | bytes 140509184 | tf_op jit(solution)/shard_map/bse,ed->bsd/dot_general | solution.py:37
  2143.6 529.1 %reduce-scatter.5.cloned.1.call-done = bf16[32,512,384]{1,2,0:T(8,128)(2,1)} async-done(((bf16[32,512,3072]{1,2,0:T(8,128)(2,1)}), bf16[32,512,384]{1,2,0:T(8,128)(2,1)}) %reduce-scatter.5.cloned.1.call-update) | async-done | bytes 12582928 | tf_op jit(solution)/shard_map/reduce_scatter | solution.py:39
  2672.7 16.7 add_convert_fusion.2
  2689.4 440.3 %all-gather.5.cloned.1.call-done = bf16[32,512,3072]{1,2,0:T(8,128)(2,1)} async-done(((bf16[32,512,384]{1,2,0:T(8,128)(2,1)}), bf16[32,512,3072]{1,2,0:T(8,128)(2,1)}) %all-gather.5.cloned.1.call-update) | async-done | bytes 100663312 | tf_op jit(solution)/shard_map/all_gather | solution.py:45
  3129.7 128.4 %copy.72 = bf16[32,512,3072]{2,1,0:T(8,128)(2,1)} copy(bf16[32,512,3072]{1,2,0:T(8,128)(2,1)} %all-gather.5.cloned.1.call-done) | data formatting | bytes 201326592 | tf_op jit(solution)/shard_map/all_gather | solution.py:45
  (113 shorter events, 11.0 us)
Async XLA Ops:
  6.5 473.0 %copy-start = (bf16[3,128,3072]{2,1,0:T(8,128)(2,1)S(1)}, bf16[3,128,3072]{2,1,0:T(8,128)(2,1)}, u32[]{:S(2)}) copy-start(bf16[3,128,3072]{2,1,0:T(8,128)(2,1)} %param.40) | copy-start | bytes 7077892
  6.5 565.4 %all-reduce.3.cloned.1.call-start = ((), (), s32[]{:S(2)}) async-start(), calls=%async_computation.3 | async-start | bytes 524288 | tf_op jit(solution)/shard_map/psum | solution.py:40
  8.0 78.5 %copy-start.20 = (pred[32]{0:T(512)(128)(4,1)}, pred[32]{0:T(512)(128)(4,1)S(1)}, u32[]{:S(2)}) copy-start(pred[32]{0:T(512)(128)(4,1)S(1)} %compare_and_fusion) | copy-start | bytes 100
  8.8 237.1 %copy-start.36 = (s32[1024]{0:T(1024)}, s32[1024]{0:T(1024)S(1)}, u32[]{:S(2)}) copy-start(s32[1024]{0:T(1024)S(1)} %pad_clamp_fusion) | copy-start | bytes 12292
  50.1 50.8 %copy-start.19 = (bf16[16,8,3,128]{3,1,2,0:T(8,128)(2,1)S(1)}, bf16[16,8,3,128]{3,1,2,0:T(8,128)(2,1)}, u32[]{:S(2)}) copy-start(bf16[16,8,3,128]{3,1,2,0:T(8,128)(2,1)} %param.45) | copy-start | bytes 294916
  50.1 56.4 %copy-start.34 = (f32[32,512]{1,0:T(8,128)S(1)}, f32[32,512]{1,0:T(8,128)}, u32[]{:S(2)}) copy-start(f32[32,512]{1,0:T(8,128)} %add_rsqrt_fusion.1) | copy-start | bytes 196612
  50.1 56.4 %copy-start.39 = (f32[3072]{0:T(1024)S(1)}, f32[3072]{0:T(1024)}, u32[]{:S(2)}) copy-start(f32[3072]{0:T(1024)} %param.35) | copy-start | bytes 36868
  106.5 48.2 %copy-start.32 = (bf16[16,8,1,128]{3,1,2,0:T(8,128)(2,1)S(1)}, bf16[16,8,1,128]{3,1,2,0:T(8,128)(2,1)}, u32[]{:S(2)}) copy-start(bf16[16,8,1,128]{3,1,2,0:T(8,128)(2,1)} %param.47) | copy-start | bytes 98308
  155.9 40.3 %copy-start.31 = (bf16[32,3072,1]{1,0,2:T(8,128)(2,1)S(1)}, bf16[32,3072,1]{1,0,2:T(8,128)(2,1)}, u32[]{:S(2)}) copy-start(bf16[32,3072,1]{1,0,2:T(8,128)(2,1)} %get-tuple-element.13) | copy-start | bytes 589828
  196.2 48.5 %copy-start.33 = (bf16[16,8,1,128]{3,1,2,0:T(8,128)(2,1)S(1)}, bf16[16,8,1,128]{3,1,2,0:T(8,128)(2,1)}, u32[]{:S(2)}) copy-start(bf16[16,8,1,128]{3,1,2,0:T(8,128)(2,1)} %param.49) | copy-start | bytes 98308
  196.2 49.7 %copy-start.4 = (bf16[16,3,128,8]{2,3,1,0:T(8,128)(2,1)S(1)}, bf16[16,3,128,8]{2,3,1,0:T(8,128)(2,1)}, u32[]{:S(2)}) copy-start(bf16[16,3,128,8]{2,3,1,0:T(8,128)(2,1)} %param.50) | copy-start | bytes 294916
  196.2 51.0 %copy-start.13 = (bf16[32,8,3,128]{3,1,2,0:T(8,128)(2,1)S(1)}, bf16[32,8,3,128]{3,1,2,0:T(8,128)(2,1)}, u32[]{:S(2)}) copy-start(bf16[32,8,3,128]{3,1,2,0:T(8,128)(2,1)} %gather_fusion) | copy-start | bytes 589828
  196.2 51.0 %copy-start.14 = (bf16[32,512,8]{1,0,2:T(8,128)(2,1)S(1)}, bf16[32,512,8]{1,0,2:T(8,128)(2,1)}, u32[]{:S(2)}) copy-start(bf16[32,512,8]{1,0,2:T(8,128)(2,1)} %all_gather.23) | copy-start | bytes 786436
  196.2 51.0 %copy-start.21 = (pred[32]{0:T(512)(128)(4,1)S(1)}, pred[32]{0:T(512)(128)(4,1)}, u32[]{:S(2)}) copy-start(pred[32]{0:T(512)(128)(4,1)} %copy-done.20) | copy-start | bytes 100
  196.2 61.9 %copy-start.35 = (f32[32,512]{1,0:T(8,128)S(1)}, f32[32,512]{1,0:T(8,128)}, u32[]{:S(2)}) copy-start(f32[32,512]{1,0:T(8,128)} %add_rsqrt_fusion.1) | copy-start | bytes 196612
  196.2 61.8 %copy-start.40 = (f32[3072]{0:T(1024)S(1)}, f32[3072]{0:T(1024)}, u32[]{:S(2)}) copy-start(f32[3072]{0:T(1024)} %param.35) | copy-start | bytes 36868
  258.1 52.3 %copy-start.6 = (pred[512,512]{0,1:T(8,128)(4,1)S(1)}, pred[512,512]{0,1:T(8,128)(4,1)}, u32[]{:S(2)}) copy-start(pred[512,512]{0,1:T(8,128)(4,1)} %iota_compare_fusion) | copy-start | bytes 786436
  258.1 52.3 %copy-start.15 = (bf16[32,512,8]{1,0,2:T(8,128)(2,1)S(1)}, bf16[32,512,8]{1,0,2:T(8,128)(2,1)}, u32[]{:S(2)}) copy-start(bf16[32,512,8]{1,0,2:T(8,128)(2,1)} %all_gather.22) | copy-start | bytes 786436
  258.1 52.3 %copy-start.29 = (bf16[32,8,128]{2,1,0:T(8,128)(2,1)S(1)}, bf16[32,8,128]{2,1,0:T(8,128)(2,1)}, u32[]{:S(2)}) copy-start(bf16[32,8,128]{2,1,0:T(8,128)(2,1)} %gather_fusion.6) | copy-start | bytes 196612
  352.1 32.3 copy-start.16
  352.1 32.3 copy-start.30
  389.1 41.2 %copy-start.28 = (f32[32,3,512]{2,1,0:T(4,128)S(1)}, f32[32,3,512]{2,1,0:T(4,128)}, u32[]{:S(2)}) copy-start(f32[32,3,512]{2,1,0:T(4,128)} %fusion.6) | copy-start | bytes 589828
  430.2 42.2 %copy-start.5 = (bf16[32,3,128,8]{2,3,1,0:T(8,128)(2,1)S(1)}, bf16[32,3,128,8]{2,3,1,0:T(8,128)(2,1)}, u32[]{:S(2)}) copy-start(bf16[32,3,128,8]{2,3,1,0:T(8,128)(2,1)} %gather_fusion.1) | copy-start | bytes 589828
  430.2 42.2 %copy-start.22 = (pred[32]{0:T(512)(128)(4,1)S(1)}, pred[32]{0:T(512)(128)(4,1)}, u32[]{:S(2)}) copy-start(pred[32]{0:T(512)(128)(4,1)} %copy-done.20) | copy-start | bytes 100
  479.5 594.3 %reduce-scatter.3.cloned.1.call-start = ((), (), s32[]{:S(2)}) async-start(), calls=%async_computation.2 | async-start | bytes 113246208 | tf_op jit(solution)/shard_map/reduce_scatter | solution.py:39
  543.1 0.9 copy-start.26
  543.1 0.9 copy-start.37
  543.1 547.5 %copy-start.17 = (bf16[16,8,1024]{2,1,0:T(8,128)(2,1)S(1)}, bf16[16,8,1024]{2,1,0:T(8,128)(2,1)}, u32[]{:S(2)}) copy-start(bf16[16,8,1024]{2,1,0:T(8,128)(2,1)} %param.55) | copy-start | bytes 786436
  543.1 548.9 %copy-start.18 = (bf16[16,8,1024]{2,1,0:T(8,128)(2,1)S(1)}, bf16[16,8,1024]{2,1,0:T(8,128)(2,1)}, u32[]{:S(2)}) copy-start(bf16[16,8,1024]{2,1,0:T(8,128)(2,1)} %param.53) | copy-start | bytes 786436
  543.1 550.2 %copy-start.2 = (bf16[16,1024,8]{1,2,0:T(8,128)(2,1)S(1)}, bf16[16,1024,8]{1,2,0:T(8,128)(2,1)}, u32[]{:S(2)}) copy-start(bf16[16,1024,8]{1,2,0:T(8,128)(2,1)} %param.56) | copy-start | bytes 786436
  543.1 987.7 %all-gather.3.cloned.1.call-start = ((), (), s32[]{:S(2)}) async-start(), calls=%async_computation.4 | async-start | bytes 113246208 | tf_op jit(solution)/shard_map/all_gather | solution.py:45
  1090.5 471.1 %copy-start.38 = (f32[3072]{0:T(1024)S(1)}, f32[3072]{0:T(1024)}, u32[]{:S(2)}) copy-start(f32[3072]{0:T(1024)} %param.36) | copy-start | bytes 36868
  1090.5 1053.0 %all-reduce.5.cloned.1.call-start = ((), (), s32[]{:S(2)}) async-start(), calls=%async_computation.6 | async-start | bytes 524288 | tf_op jit(solution)/shard_map/psum | solution.py:40
  1561.6 65.6 %copy-start.10 = (bf16[32,3072,1]{1,0,2:T(8,128)(2,1)S(1)}, bf16[32,3072,1]{1,0,2:T(8,128)(2,1)}, u32[]{:S(2)}) copy-start(bf16[32,3072,1]{1,0,2:T(8,128)(2,1)} %get-tuple-element.6) | copy-start | bytes 589828
  1627.2 43.4 %copy-start.9 = (bf16[32,3072,1]{1,0,2:T(8,128)(2,1)S(1)}, bf16[32,3072,1]{1,0,2:T(8,128)(2,1)}, u32[]{:S(2)}) copy-start(bf16[32,3072,1]{1,0,2:T(8,128)(2,1)} %get-tuple-element.12) | copy-start | bytes 589828
  1713.9 116.6 %copy-start.8 = (bf16[32,8,1024]{2,1,0:T(8,128)(2,1)S(1)}, bf16[32,8,1024]{2,1,0:T(8,128)(2,1)}, u32[]{:S(2)}) copy-start(bf16[32,8,1024]{2,1,0:T(8,128)(2,1)} %gather_fusion.12) | copy-start | bytes 1572868
  1713.9 116.6 %copy-start.11 = (bf16[32,512,8]{1,0,2:T(8,128)(2,1)S(1)}, bf16[32,512,8]{1,0,2:T(8,128)(2,1)}, u32[]{:S(2)}) copy-start(bf16[32,512,8]{1,0,2:T(8,128)(2,1)} %all_gather.26) | copy-start | bytes 786436
  1713.9 116.6 %copy-start.23 = (pred[32]{0:T(512)(128)(4,1)S(1)}, pred[32]{0:T(512)(128)(4,1)}, u32[]{:S(2)}) copy-start(pred[32]{0:T(512)(128)(4,1)} %copy-done.20) | copy-start | bytes 100
  1830.5 23.3 copy-start.7
  1830.5 23.3 copy-start.12
  1876.9 135.4 %copy-start.3 = (bf16[32,1024,8]{1,2,0:T(8,128)(2,1)S(1)}, bf16[32,1024,8]{1,2,0:T(8,128)(2,1)}, u32[]{:S(2)}) copy-start(bf16[32,1024,8]{1,2,0:T(8,128)(2,1)} %gather_fusion.2) | copy-start | bytes 1572868
  1876.9 135.4 %copy-start.24 = (pred[32]{0:T(512)(128)(4,1)S(1)}, pred[32]{0:T(512)(128)(4,1)}, u32[]{:S(2)}) copy-start(pred[32]{0:T(512)(128)(4,1)} %copy-done.20) | copy-start | bytes 100
  2027.1 645.6 %reduce-scatter.5.cloned.1.call-start = ((), (), s32[]{:S(2)}) async-start(), calls=%async_computation.5 | async-start | bytes 113246208 | tf_op jit(solution)/shard_map/reduce_scatter | solution.py:39
  2141.9 0.9 copy-start.27
  2141.9 530.7 %copy-start.25 = (pred[32]{0:T(512)(128)(4,1)S(1)}, pred[32]{0:T(512)(128)(4,1)}, u32[]{:S(2)}) copy-start(pred[32]{0:T(512)(128)(4,1)} %copy-done.20) | copy-start | bytes 100
  2142.0 987.7 %all-gather.5.cloned.1.call-start = ((), (), s32[]{:S(2)}) async-start(), calls=%async_computation.7 | async-start | bytes 113246208 | tf_op jit(solution)/shard_map/all_gather | solution.py:45
  2689.4 568.7 %copy-start.1 = (bf16[3,128,3072]{2,1,0:T(8,128)(2,1)S(1)}, bf16[3,128,3072]{2,1,0:T(8,128)(2,1)}, u32[]{:S(2)}) copy-start(bf16[3,128,3072]{2,1,0:T(8,128)(2,1)} %param.40) | copy-start | bytes 7077892
Sparse Core Ops, SparseCore 0:
  479.6 42.5 all-reduce.2
  543.2 530.5 reduce-scatter.2
  1090.6 440.1 all-gather.2
  2027.2 42.5 all-reduce.4
  2142.1 530.5 reduce-scatter.4
  2689.5 440.1 all-gather.4
where the time goes:
time: 3280 us; the launch traced here: 3270 us
  waiting for transfers between devices  1910 us (58%)
  matrix products  938 us (29%)
  local copies, waits for them, and re-layouts  181 us (6%)
  other arithmetic  163 us (5%)
  blocking collectives  61.3 us (2%)
    reduce_scatter x2, waiting for transfers between devices, row_proj(): lax.psum_scatter(base_part, 'tp', scatter_dimension=2, tiled=True)  1030 us
    all_gather x2, waiting for transfers between devices, row_proj(): lax.all_gather(out_loc.astype(jnp.bfloat16), 'tp', axis=2, tiled=True)  876 us
    dot_general x5, matrix products, column_proj(): jnp.einsum('bsd,de->bse', h_in, w_loc, preferred_element_type=jnp.float32)  386 us
    dot_general x2, matrix products, row_proj(): jnp.einsum('bse,ed->bsd', h_in, w_loc, preferred_element_type=jnp.float32)  178 us
    dot_general x5, matrix products, column_proj(): jnp.einsum('bsd,bdr->bsr', h_in, a_sel, preferred_element_type=jnp.float32)  173 us
    all_gather x1, local copies, waits for them, and re-layouts, row_proj(): lax.all_gather(out_loc.astype(jnp.bfloat16), 'tp', axis=2, tiled=True)  128 us
  transfers between devices with their start and end apart: 6, of which 4 were waited for; matrix products, arithmetic and copies ran while one was open for 6% of the time, Pallas kernels for 0%

commit v1 on v0

v1 whole, which is shorter than its diff:
```python
import jax
import jax.numpy as jnp
from jax import lax
from jax.sharding import PartitionSpec as P

LORA_ALPHA = 16
RMS_EPS = 1e-5


def rms_scale(x_in, gain_vec):
    x_f32 = x_in.astype(jnp.float32)
    inv_rms = lax.rsqrt(jnp.mean(x_f32 * x_f32, axis=-1, keepdims=True) + RMS_EPS)
    return (x_f32 * inv_rms * gain_vec).astype(jnp.bfloat16)


def causal_attention(q_group, k_group, v_group):
    num_seqs, seq_len, head_dim = q_group.shape[0], q_group.shape[1], q_group.shape[-1]
    scores = jnp.einsum('bqngd,bknd->bngqk', q_group, k_group, preferred_element_type=jnp.float32) * head_dim ** -0.5
    causal = jnp.arange(seq_len)[:, None] >= jnp.arange(seq_len)[None, :]
    prob_bf = jax.nn.softmax(jnp.where(causal, scores, -jnp.inf), axis=-1).astype(jnp.bfloat16)
    att_out = jnp.einsum('bngqk,bknd->bqngd', prob_bf, v_group, preferred_element_type=jnp.float32)
    return att_out.astype(jnp.bfloat16)


def solution(mesh):
    act_spec = P('dp', None, None)
    w_head_spec = P(None, 'tp', None)
    w_out_spec = P('tp', None, None)
    w_col_spec = P(None, 'tp')
    w_row_spec = P('tp', None)
    a_rank_spec = P(None, None, 'tp')
    b_head_spec = P(None, None, 'tp', None)
    b_col_spec = P(None, None, 'tp')
    a_head_spec = P(None, 'tp', None, None)
    a_row_spec = P(None, 'tp', None)
    in_specs = (act_spec, P('dp'), P(None), P(None), w_head_spec, w_head_spec, w_head_spec, w_out_spec,
                w_col_spec, w_col_spec, w_row_spec, a_rank_spec, b_head_spec, a_rank_spec, b_head_spec,
                a_rank_spec, b_head_spec, a_head_spec, b_col_spec, a_rank_spec, b_col_spec,
                a_rank_spec, b_col_spec, a_row_spec, b_col_spec)
    n_tp = mesh.shape['tp']

    def local_layer(x_in, adapter_ids, gain_attn, gain_mlp, w_q, w_k, w_v, w_o, w_gate, w_up, w_down,
                    a_q, b_q, a_k, b_k, a_v, b_v, a_o, b_o, a_gate, b_gate, a_up, b_up, a_down, b_down):
        num_seqs, seq_len, dim = x_in.shape
        head_dim = w_q.shape[2]
        rank = b_q.shape[1]
        scale = LORA_ALPHA / rank
        n_ad = b_q.shape[0]
        per_dev = num_seqs // n_tp
        me = lax.axis_index('tp')
        x_loc = lax.dynamic_slice_in_dim(x_in, me * per_dev, per_dev, axis=0)
        ids = lax.dynamic_slice_in_dim(adapter_ids, me * per_dev, per_dev, axis=0)

        def gather(v):
            return lax.all_gather(v, 'tp', axis=0, tiled=False)

        def t_last(a):
            return jnp.swapaxes(a, -1, -2)

        qw, kw = w_q.shape[1] * head_dim, w_k.shape[1] * head_dim
        lora_attn = gather(jnp.concatenate([
            b_q.reshape(n_ad, rank, qw), b_k.reshape(n_ad, rank, kw), b_v.reshape(n_ad, rank, kw),
            t_last(a_o.reshape(n_ad, qw, rank)), b_o], axis=2))
        lora_a = gather(jnp.stack([a_q[:, :, 0], a_k[:, :, 0], a_v[:, :, 0], a_gate[:, :, 0], a_up[:, :, 0]], axis=0))
        w_qkv_all = gather(jnp.concatenate([w_q.reshape(dim, qw), w_k.reshape(dim, kw), w_v.reshape(dim, kw)], axis=1))
        w_o_all = gather(w_o.reshape(qw, dim))
        w_gate_all = gather(w_gate)
        w_up_all = gather(w_up)
        w_down_all = gather(w_down)
        lora_mlp = gather(jnp.concatenate([b_gate, b_up, t_last(a_down), b_down], axis=2))

        lora_attn = jnp.take(lora_attn, ids, axis=1)
        lora_mlp = jnp.take(lora_mlp, ids, axis=1)
        lora_a = jnp.take(lora_a, ids, axis=2)

        f32 = jnp.float32
        h = rms_scale(x_loc, gain_attn)
        t_qkv = jnp.einsum('bsd,rpbd->bspr', h, lora_a[:, :3], preferred_element_type=f32).astype(jnp.bfloat16)

        def col(h_in, w_all, t_in, b_all):
            z = jnp.einsum('bsd,gde->bsge', h_in, w_all, preferred_element_type=f32)
            return z + scale * jnp.einsum('bsr,gbre->bsge', t_in, b_all, preferred_element_type=f32)

        q = col(h, w_qkv_all[:, :, :qw], t_qkv[:, :, 0], lora_attn[..., :qw]).astype(jnp.bfloat16)
        k = col(h, w_qkv_all[:, :, qw:qw + kw], t_qkv[:, :, 1], lora_attn[..., qw:qw + kw]).astype(jnp.bfloat16)
        v = col(h, w_qkv_all[:, :, qw + kw:], t_qkv[:, :, 2], lora_attn[..., qw + kw:qw + 2 * kw]).astype(jnp.bfloat16)
        q = q.reshape(per_dev, seq_len, n_tp, qw // head_dim, head_dim)
        o = causal_attention(q, k, v).reshape(per_dev, seq_len, n_tp, qw)

        def row(u, w_all, a_t, b_all, resid):
            z = jnp.einsum('bsge,gef->bsf', u, w_all, preferred_element_type=f32)
            t = jnp.einsum('bsge,gbre->bsr', u, a_t, preferred_element_type=f32).astype(jnp.bfloat16)
            bb = jnp.moveaxis(b_all, 0, 2).reshape(per_dev, rank, dim)
            z = z + scale * jnp.einsum('bsr,brf->bsf', t, bb, preferred_element_type=f32)
            return (resid.astype(f32) + z).astype(jnp.bfloat16)

        off = qw + 2 * kw
        x_one = row(o, w_o_all, lora_attn[..., off:off + qw], lora_attn[..., off + qw:], x_loc)
        h2 = rms_scale(x_one, gain_mlp)
        t_gu = jnp.einsum('bsd,rpbd->bspr', h2, lora_a[:, 3:], preferred_element_type=f32).astype(jnp.bfloat16)
        ff = w_gate.shape[1]
        gate = col(h2, w_gate_all, t_gu[:, :, 0], lora_mlp[..., :ff]).astype(jnp.bfloat16)
        up = col(h2, w_up_all, t_gu[:, :, 1], lora_mlp[..., ff:2 * ff]).astype(jnp.bfloat16)
        mid = (jax.nn.silu(gate.astype(f32)) * up.astype(f32)).astype(jnp.bfloat16)
        y = row(mid, w_down_all, lora_mlp[..., 2 * ff:3 * ff], lora_mlp[..., 3 * ff:], x_one)
        return lax.all_gather(y, 'tp', axis=0, tiled=True)

    return jax.shard_map(local_layer, mesh=mesh, in_specs=in_specs, out_specs=act_spec, check_vma=False)
```

time: 3280 us -> 1790 us (0.55)
  waiting for transfers between devices: 1910 us -> 778 us
  other arithmetic: 163 us -> 13.6 us
  matrix products: 938 us -> 838 us
  blocking collectives: 61.3 us -> 0 us
  local copies, waits for them, and re-layouts: 181 us -> 140 us
    reduce_scatter x2 -> x0, waiting for transfers between devices: 1030 us -> none  [row_proj(): lax.psum_scatter(base_part, 'tp', scatter_dimension=2, tiled=True)]
    dot_general x21 -> x15, matrix products: 895 us -> 750 us  [the longest x5 352 us: col(): z = jnp.einsum('bsd,gde->bsge', h_in, w_all, preferred_element_type=f32)]
    all_gather x2 -> x9, waiting for transfers between devices: 876 us -> 776 us  [the longest x1 439 us: local_layer(): return lax.all_gather(y, 'tp', axis=0, tiled=True)]
    all_gather x1 -> x2, local copies, waits for them, and re-layouts: 128 us -> 46.7 us  [gather(): return lax.all_gather(v, 'tp', axis=0, tiled=False)]
    convert_element_type x1 -> x0, other arithmetic: 65.6 us -> none  [rms_scale(): return (x_f32 * inv_rms * gain_vec).astype(jnp.bfloat16)]
    all_gather x5 -> x0, blocking collectives: 61.3 us -> none  [column_proj(): value_a8 = lax.all_gather(value_a9, 'tp', axis=2, tiled=True)]
    unnamed x84 -> x40, local copies, waits for them, and re-layouts: 22.7 us -> 82.2 us
    reduce_sum x2 -> x1, other arithmetic: 61.6 us -> 7.1 us  [rms_scale(): jnp.mean(x_f32 * x_f32, axis=-1, keepdims=True) + RMS_EPS]
  transfers between devices with their start and end apart: 6 -> 9, of which waited for: 4 -> 7; matrix products, arithmetic and copies ran while one was open for 6% -> 39% of each run, Pallas kernels for 0% -> 0%
where the time goes in v1:
time: 1790 us; the launch traced here: 1780 us
  matrix products  838 us (47%)
  waiting for transfers between devices  778 us (43%)
  local copies, waits for them, and re-layouts  140 us (8%)
    all_gather x1, waiting for transfers between devices, local_layer(): return lax.all_gather(y, 'tp', axis=0, tiled=True)  439 us
    dot_general x5, matrix products, col(): z = jnp.einsum('bsd,gde->bsge', h_in, w_all, preferred_element_type=f32)  352 us
    all_gather x8, waiting for transfers between devices, gather(): return lax.all_gather(v, 'tp', axis=0, tiled=False)  337 us
    dot_general x2, matrix products, row(): z = jnp.einsum('bsge,gef->bsf', u, w_all, preferred_element_type=f32)  276 us
    unnamed x40, local copies, waits for them, and re-layouts  82.2 us
    dot_general x4, matrix products, col(): jnp.einsum('bsr,gbre->bsge', t_in, b_all, preferred_element_type=f32)  60.6 us
    sub x1, matrix products, causal_attention(): jax.nn.softmax(jnp.where(causal, scores, -jnp.inf), axis=-1)  48.2 us
    all_gather x2, local copies, waits for them, and re-layouts, gather(): return lax.all_gather(v, 'tp', axis=0, tiled=False)  46.7 us
  transfers between devices with their start and end apart: 9, of which 7 were waited for; matrix products, arithmetic and copies ran while one was open for 39% of the time, Pallas kernels for 0%

profile of v1, /device:TPU:0, one launch (start us, length us, event | category | flops | bytes accessed | tf_op | source)
XLA Modules:
  0.0 1783.6 jit_solution(17610844315264191556)
XLA Ops:
  6.5 0.9 bitcast_dynamic-update-slice_fusion.1
  7.5 0.8 bitcast_dynamic-update-slice_fusion.8
  8.2 0.8 bitcast_dynamic-update-slice_fusion.7
  9.0 0.9 bitcast_dynamic-update-slice_fusion
  9.9 0.9 constant_dynamic-update-slice_fusion
  11.6 0.9 bitcast_dynamic-update-slice_fusion.6
  12.5 0.9 bitcast_dynamic-update-slice_fusion.5
  13.4 0.9 bitcast_dynamic-update-slice_fusion.4
  14.3 0.9 bitcast_dynamic-update-slice_fusion.3
  15.2 0.9 bitcast_dynamic-update-slice_fusion.2
  16.1 0.8 copy-done.6
  17.0 2.1 pad_maximum_fusion.1
  19.2 2.8 copy.50
  22.0 1.4 copy.51
  23.5 2.3 copy.52
  25.7 3.0 pad_maximum_fusion
  31.5 0.8 iota_compare_fusion
  32.4 7.1 fusion.11
  39.8 2.5 gather_fusion.1
  42.4 28.9 %all-gather.23.cloned.1.call-done = bf16[40,16,3072]{2,1,0:T(8,128)(2,1)} async-done(((bf16[5,16,3072]{2,1,0:T(8,128)(2,1)}), bf16[40,16,3072]{2,1,0:T(8,128)(2,1)}) %all-gather.23.cloned.1.call-update) | async-done | bytes 3932176 | tf_op jit(solution)/shard_map/all_gather | solution.py:55
  71.3 6.2 copy.54
  77.5 2.7 gather_fusion
  80.3 6.8 fusion.35
  87.1 10.1 fusion.53
  97.2 18.8 %all-gather.29.cloned.1.call-done = bf16[128,8,3456]{2,1,0:T(8,128)(2,1)} async-done(((bf16[16,8,3456]{2,1,0:T(8,128)(2,1)}), bf16[128,8,3456]{2,1,0:T(8,128)(2,1)}) %all-gather.29.cloned.1.call-update) | async-done | bytes 7077904 | tf_op jit(solution)/shard_map/all_gather | solution.py:55
  116.0 3.8 gather_fusion.2
  120.1 1.3 copy-done
  121.4 142.7 %all-gather.21.cloned.1.call-done = bf16[24576,640]{0,1:T(8,128)(2,1)} async-done(((bf16[3072,640]{0,1:T(8,128)(2,1)}), bf16[24576,640]{0,1:T(8,128)(2,1)}) %all-gather.21.cloned.1.call-update) | async-done | bytes 31457296 | tf_op jit(solution)/shard_map/all_gather | solution.py:55
  264.0 40.5 %copy.53 = bf16[24576,640]{1,0:T(8,128)(2,1)} copy(bf16[24576,640]{0,1:T(8,128)(2,1)} %all-gather.21.cloned.1.call-done) | data formatting | bytes 62914560 | tf_op jit(solution)/shard_map/all_gather | solution.py:55
  304.6 17.7 fusion.27
  322.2 19.1 %fusion.28 = f32[4,512,8,128]{3,1,2,0:T(8,128)} fusion(bf16[8,3072,640]{2,1,0:T(8,128)(2,1)} %bitcast.200, f32[3072]{0:T(1024)S(1)} %copy-done.12, f32[4,512]{1,0:T(4,128)S(1)} %add_rsqrt_fusion.1, bf16[32,512,3072]{2,1,0:T(8,128)(2,1)} %param.25, s32[]{:T(128)S(6)} %select_n.29), kind=kOutput, calls=%fused_computation.51 | convolution fusion | flops 12910067712 | bytes 27283460 | tf_op jit(solution)/shard_map/bsd,gde->bsge/dot_general | solution.py:81
  341.3 3.2 fusion.31
  344.5 52.0 %add_convert_fusion.2 = bf16[4,512,8,384]{1,3,2,0:T(8,128)(2,1)} fusion(f32[4,512,8,384]{1,3,2,0:T(8,128)} %fusion.53, bf16[8,3072,640]{2,1,0:T(8,128)(2,1)} %bitcast.201, f32[3072]{0:T(1024)S(1)} %copy-done.12, f32[4,512]{1,0:T(4,128)S(1)} %add_rsqrt_fusion.1, bf16[32,512,3072]{2,1,0:T(8,128)(2,1)} %param.25, s32[]{:T(128)S(6)} %select_n.29), kind=kOutput, calls=%fused_computation.37 | convolution fusion | flops 38698745856 | bytes 69226496 | tf_op jit(solution)/shard_map/bsd,gde->bsge/dot_general | solution.py:81
  396.5 48.2 %fusion.67 = (f32[4,8,3,512]{3,2,1,0:T(4,128)S(1)}, f32[4,8,3,512,512]{3,4,2,1,0:T(8,128)}) fusion(pred[512,512]{0,1:T(8,128)(4,1)S(1)} %copy-done.8, bf16[4,512,8,128,1]{3,1,4,2,0:T(8,128)(2,1)} %fusion.31, bf16[4,512,8,3,128]{1,4,3,2,0:T(8,128)(2,1)} %bitcast.217), kind=kOutput, calls=%fused_computation.108 | convolution fusion | flops 6543114752 | bytes 117899264 | tf_op jit(solution)/shard_map/sub | solution.py:20
  444.8 39.8 %fusion.26 = bf16[4,8,128,3,512]{4,2,3,1,0:T(8,128)(2,1)} fusion(f32[4,8,3,512,512]{3,4,2,1,0:T(8,128)} %get-tuple-element.8, f32[4,8,3,512]{3,2,1,0:T(4,128)S(1)} %get-tuple-element.7, f32[4,512,8,128]{3,1,2,0:T(8,128)} %fusion.28, bf16[8,4,8,1408]{3,2,0,1:T(8,128)(2,1)S(1)} %select_bitcast_fusion.1, bf16[4,512,3,8]{1,3,2,0:T(8,128)(2,1)S(1)} %fusion.35), kind=kOutput, calls=%fused_computation.47 | convolution fusion | flops 6538919936 | bytes 121995264 | tf_op jit(solution)/shard_map/bngqk,bknd->bqngd/dot_general | solution.py:21
  484.6 48.5 %fusion.20 = f32[4,512,3072,1]{2,1,3,0:T(8,128)} fusion(bf16[4,512,8,384]{1,3,2,0:T(8,128)(2,1)} %bitcast.202, bf16[8,384,3072]{2,1,0:T(8,128)(2,1)} %all-gather.17.cloned.1.call-done), kind=kOutput, calls=%fused_computation.40 | convolution fusion | flops 38654705664 | bytes 56623104 | tf_op jit(solution)/shard_map/bsge,gef->bsf/dot_general | solution.py:91
  533.1 22.8 %fusion.15 = (f32[4,512]{1,0:T(4,128)S(1)}, bf16[4,512,3072]{2,1,0:T(8,128)(2,1)}) fusion(bf16[4,8,3072]{2,1,0:T(8,128)(2,1)S(1)} %bitcast.209, bf16[4,512,8,384]{1,3,2,0:T(8,128)(2,1)} %bitcast.203, bf16[8,4,8,1408]{3,2,0,1:T(8,128)(2,1)S(1)} %copy-done.4, f32[4,512,3072,1]{2,1,3,0:T(8,128)} %fusion.20, bf16[32,512,3072]{2,1,0:T(8,128)(2,1)} %param.25, ...), kind=kOutput, calls=%fused_computation.31 | convolution fusion | flops 251672576 | bytes 63315972 | tf_op jit(solution)/shard_map/bsr,brf->bsf/dot_general | solution.py:94
  555.9 8.2 fusion.36
  564.1 24.2 %fusion.49 = f32[4,512,8,1024]{3,1,2,0:T(8,128)} fusion(bf16[8,4,8,3456]{3,2,0,1:T(8,128)(2,1)S(1)} %copy-done.1, bf16[4,512,2,8]{1,3,2,0:T(8,128)(2,1)S(1)} %fusion.36), kind=kOutput, calls=%fused_computation.76 | convolution fusion | flops 268435456 | bytes 67665920 | tf_op jit(solution)/shard_map/bsr,gbre->bsge/dot_general | solution.py:82
  588.3 23.1 %fusion.47 = f32[4,512,8,1024]{3,1,2,0:T(8,128)} fusion(bf16[8,4,8,3456]{3,2,0,1:T(8,128)(2,1)S(1)} %copy-done.1, bf16[4,512,2,8]{1,3,2,0:T(8,128)(2,1)S(1)} %fusion.36), kind=kOutput, calls=%fused_computation.74 | convolution fusion | flops 268435456 | bytes 67665920 | tf_op jit(solution)/shard_map/bsr,gbre->bsge/dot_general | solution.py:82
  611.4 124.0 %add_convert_fusion.1 = bf16[4,512,8,1024]{3,1,2,0:T(8,128)(2,1)} fusion(f32[4,512,8,1024]{3,1,2,0:T(8,128)} %fusion.49, bf16[8,3072,1024,1]{2,1,0,3:T(8,128)(2,1)} %bitcast.215, bf16[4,512,3072]{2,1,0:T(8,128)(2,1)} %get-tuple-element.10, f32[3072]{0:T(1024)S(1)} %copy-done.13, f32[4,512]{1,0:T(4,128)S(1)} %add_rsqrt_fusion), kind=kOutput, calls=%fused_computation.15 | convolution fusion | flops 103154712576 | bytes 163598336 | tf_op jit(solution)/shard_map/bsd,gde->bsge/dot_general | solution.py:81
  735.5 80.1 %all-gather.31.cloned.1.call-done = bf16[24576,1024]{1,0:T(8,128)(2,1)} async-done(((bf16[3072,1024]{1,0:T(8,128)(2,1)}), bf16[24576,1024]{1,0:T(8,128)(2,1)}) %all-gather.31.cloned.1.call-update) | async-done | bytes 50331664 | tf_op jit(solution)/shard_map/all_gather | solution.py:55
  815.5 138.8 %fusion.6 = bf16[4,512,8,1024]{3,1,2,0:T(8,128)(2,1)} fusion(bf16[4,512,8,1024]{3,1,2,0:T(8,128)(2,1)} %add_convert_fusion.1, f32[4,512,8,1024]{3,1,2,0:T(8,128)} %fusion.47, bf16[8,3072,1024,1]{2,1,0,3:T(8,128)(2,1)} %bitcast.216, bf16[4,512,3072]{2,1,0:T(8,128)(2,1)} %get-tuple-element.10, f32[3072]{0:T(1024)S(1)} %copy-done.13, ...), kind=kOutput, calls=%fused_computation.16 | convolution fusion | flops 103288930304 | bytes 197152768 | tf_op jit(solution)/shard_map/bsd,gde->bsge/dot_general | solution.py:81
  954.3 23.9 %fusion.39 = f32[4,512,3072]{2,1,0:T(8,128)} fusion(bf16[4,8,3072]{2,1,0:T(8,128)(2,1)S(1)} %bitcast.204, bf16[4,512,8,1024]{3,1,2,0:T(8,128)(2,1)} %fusion.6, bf16[8,4,8,3456]{3,2,0,1:T(8,128)(2,1)S(1)} %copy-done.2), kind=kOutput, calls=%fused_computation.66 | convolution fusion | flops 369115136 | bytes 59441152 | tf_op jit(solution)/shard_map/bsr,brf->bsf/dot_general | solution.py:94
  978.2 65.8 %all-gather.33.cloned.1.call-done = bf16[8192,3072]{1,0:T(8,128)(2,1)} async-done(((bf16[1024,3072]{1,0:T(8,128)(2,1)}), bf16[8192,3072]{1,0:T(8,128)(2,1)}) %all-gather.33.cloned.1.call-update) | async-done | bytes 50331664 | tf_op jit(solution)/shard_map/all_gather | solution.py:55
  1044.0 227.6 %fusion.18 = bf16[4,512,3072]{2,1,0:T(8,128)(2,1)} fusion(bf16[4,512,3072]{2,1,0:T(8,128)(2,1)} %get-tuple-element.10, f32[4,512,3072]{2,1,0:T(8,128)} %fusion.39, bf16[4,512,8,1024]{3,1,2,0:T(8,128)(2,1)} %fusion.6, bf16[8,1024,3072,1]{2,1,0,3:T(8,128)(2,1)} %bitcast.214), kind=kOutput, calls=%fused_computation.34 | convolution fusion | flops 103110672384 | bytes 134217728 | tf_op jit(solution)/shard_map/bsge,gef->bsf/dot_general | solution.py:91
  1271.7 439.3 %all-gather.19.cloned.1.call-done = bf16[32,512,3072]{2,1,0:T(8,128)(2,1)} async-done(((bf16[4,512,3072]{2,1,0:T(8,128)(2,1)}), bf16[32,512,3072]{2,1,0:T(8,128)(2,1)}) %all-gather.19.cloned.1.call-update) | async-done | bytes 100663312 | tf_op jit(solution)/shard_map/all_gather | solution.py:106
  1711.0 65.9 %copy.90 = bf16[32,512,3072]{2,1,0:T(8,128)(2,1)} copy(bf16[32,512,3072]{2,1,0:T(8,128)(2,1)} %all-gather.19.cloned.1.call-done) | data formatting | bytes 201326592
  (57 shorter events, 4.4 us)
Async XLA Ops:
  6.5 25.8 %copy-start.11 = (s32[32]{0:T(128)S(1)}, s32[32]{0:T(128)}, u32[]{:S(2)}) copy-start(s32[32]{0:T(128)} %param.26) | copy-start | bytes 388
  6.5 33.3 %all-gather.25.cloned.1.call-start = ((), (), s32[]{:S(2)}) async-start(), calls=%async_computation.4 | async-start | bytes 3244032 | tf_op jit(solution)/shard_map/all_gather | solution.py:55
  10.8 0.7 copy-start.7
  11.6 59.7 %all-gather.23.cloned.1.call-start = ((), (), s32[]{:S(2)}) async-start(), calls=%async_computation.3 | async-start | bytes 4423680 | tf_op jit(solution)/shard_map/all_gather | solution.py:55
  16.1 0.8 copy-start.6
  16.9 99.1 %all-gather.29.cloned.1.call-start = ((), (), s32[]{:S(2)}) async-start(), calls=%async_computation.6 | async-start | bytes 7962624 | tf_op jit(solution)/shard_map/all_gather | solution.py:55
  19.1 244.9 %all-gather.21.cloned.1.call-start = ((), (), s32[]{:S(2)}) async-start(), calls=%async_computation.2 | async-start | bytes 35389440 | tf_op jit(solution)/shard_map/all_gather | solution.py:55
  28.8 51.5 %copy-start.12 = (f32[3072]{0:T(1024)S(1)}, f32[3072]{0:T(1024)}, u32[]{:S(2)}) copy-start(f32[3072]{0:T(1024)} %param.27) | copy-start | bytes 36868
  28.8 455.8 %all-gather.17.cloned.1.call-start = ((), (), s32[]{:S(2)}) async-start(), calls=%async_computation | async-start | bytes 21233664 | tf_op jit(solution)/shard_map/all_gather | solution.py:55
  29.4 582.0 %all-gather.27.cloned.1.call-start = ((), (), s32[]{:S(2)}) async-start(), calls=%async_computation.5 | async-start | bytes 56623104 | tf_op jit(solution)/shard_map/all_gather | solution.py:55
  30.0 785.5 %all-gather.31.cloned.1.call-start = ((), (), s32[]{:S(2)}) async-start(), calls=%async_computation.7 | async-start | bytes 56623104 | tf_op jit(solution)/shard_map/all_gather | solution.py:55
  30.7 1013.3 %all-gather.33.cloned.1.call-start = ((), (), s32[]{:S(2)}) async-start(), calls=%async_computation.8 | async-start | bytes 56623104 | tf_op jit(solution)/shard_map/all_gather | solution.py:55
  31.5 1679.5 %all-gather.19.cloned.1.call-start = ((), (), s32[]{:S(2)}) async-start(), calls=%async_computation.1 | async-start | bytes 113246208 | tf_op jit(solution)/shard_map/all_gather | solution.py:106
  32.4 87.4 %copy-start.9 = (pred[4]{0:T(512)(128)(4,1)}, pred[4]{0:T(512)(128)(4,1)S(1)}, u32[]{:S(2)}) copy-start(pred[4]{0:T(512)(128)(4,1)S(1)} %get-tuple-element.5) | copy-start | bytes 16
  42.4 402.3 %copy-start.3 = (bf16[8,4,8,1408]{3,2,0,1:T(8,128)(2,1)}, bf16[8,4,8,1408]{3,2,0,1:T(8,128)(2,1)S(1)}, u32[]{:S(2)}) copy-start(bf16[8,4,8,1408]{3,2,0,1:T(8,128)(2,1)S(1)} %select_bitcast_fusion.1) | copy-start | bytes 2162692
  80.2 35.7 %copy-start.5 = (bf16[4,8,5,3072]{3,1,2,0:T(8,128)(2,1)}, bf16[4,8,5,3072]{3,1,2,0:T(8,128)(2,1)S(1)}, u32[]{:S(2)}) copy-start(bf16[4,8,5,3072]{3,1,2,0:T(8,128)(2,1)S(1)} %gather_fusion) | copy-start | bytes 2949124
  120.1 1.3 copy-start
  344.5 52.0 %copy-start.8 = (pred[512,512]{0,1:T(8,128)(4,1)S(1)}, pred[512,512]{0,1:T(8,128)(4,1)}, u32[]{:S(2)}) copy-start(pred[512,512]{0,1:T(8,128)(4,1)} %iota_compare_fusion) | copy-start | bytes 786436
  484.6 48.5 %copy-start.4 = (bf16[8,4,8,1408]{3,2,0,1:T(8,128)(2,1)S(1)}, bf16[8,4,8,1408]{3,2,0,1:T(8,128)(2,1)}, u32[]{:S(2)}) copy-start(bf16[8,4,8,1408]{3,2,0,1:T(8,128)(2,1)} %copy-done.3) | copy-start | bytes 2162692
  484.6 48.5 %slice-start.1 = ((bf16[8,4,8,1408]{3,2,0,1:T(8,128)(2,1)}), bf16[8,4,8,384]{3,2,0,1:T(8,128)(2,1)S(1)}, s32[]{:S(2)}) async-start(bf16[8,4,8,1408]{3,2,0,1:T(8,128)(2,1)} %copy-done.3), calls=%async_computation.10 | async-start | bytes 393216 | tf_op jit(solution)/shard_map/slice | solution.py:98
  533.1 22.8 %copy-start.10 = (pred[4]{0:T(512)(128)(4,1)S(1)}, pred[4]{0:T(512)(128)(4,1)}, u32[]{:S(2)}) copy-start(pred[4]{0:T(512)(128)(4,1)} %copy-done.9) | copy-start | bytes 16
  533.1 22.8 %copy-start.13 = (f32[3072]{0:T(1024)S(1)}, f32[3072]{0:T(1024)}, u32[]{:S(2)}) copy-start(f32[3072]{0:T(1024)} %param.28) | copy-start | bytes 36868
  533.1 31.0 %copy-start.1 = (bf16[8,4,8,3456]{3,2,0,1:T(8,128)(2,1)S(1)}, bf16[8,4,8,3456]{3,2,0,1:T(8,128)(2,1)}, u32[]{:S(2)}) copy-start(bf16[8,4,8,3456]{3,2,0,1:T(8,128)(2,1)} %copy-done) | copy-start | bytes 5308420
  815.5 138.8 %copy-start.2 = (bf16[8,4,8,3456]{3,2,0,1:T(8,128)(2,1)S(1)}, bf16[8,4,8,3456]{3,2,0,1:T(8,128)(2,1)}, u32[]{:S(2)}) copy-start(bf16[8,4,8,3456]{3,2,0,1:T(8,128)(2,1)} %copy-done) | copy-start | bytes 5308420
  815.5 138.8 %slice-start = ((bf16[8,4,8,3456]{3,2,0,1:T(8,128)(2,1)}), bf16[8,4,8,384]{3,2,0,1:T(8,128)(2,1)S(1)}, s32[]{:S(2)}) async-start(bf16[8,4,8,3456]{3,2,0,1:T(8,128)(2,1)} %copy-done), calls=%async_computation.9 | async-start | bytes 393216 | tf_op jit(solution)/shard_map/slice | solution.py:105
Sparse Core Ops, SparseCore 0:
  11.7 28.0 all-gather.24
  41.6 29.6 all-gather.22
  73.1 42.8 all-gather.28
  117.7 146.3 all-gather.20
  265.7 92.9 all-gather.16
  360.4 226.6 all-gather.26
  588.9 226.6 all-gather.30
  817.4 226.5 all-gather.32
  1271.8 439.1 all-gather.18
